TPU v7x, 128 devices: a whole 4x4x4 slice. The times are simulated.
128 devices in a mesh: dp: 8 (over x, y_lo), vocab: 16 (over z, y_hi, core).
Axes of the slice: x: 4, y: 4 (y_hi: 2, y_lo: 2; y = y_hi * 2 + y_lo), z: 4, core: 2. Of those that a mesh axis runs over, the one named last changes fastest.
Arguments:
- hidden: bfloat16 [8192, 5120], P(('dp', 'vocab')), may hold values from -100 to 100
- tokens: int32 [8192], P('dp'), may hold values from 0 to 18431
- old_weight: bfloat16 [18432, 5120], P('vocab'), may hold values from -1 to 1
- new_weight: bfloat16 [18432, 5120], P('dp', 'vocab'), may hold values from -6 to 6
Outputs:
- logprob: float32 [8192], P(('dp', 'vocab'))
- engine_weight: bfloat16 [18432, 5120], P('vocab')
All inputs are finite; a program needn't handle non-finite values.
Results may differ from a plain program's by a relative error of at most 0.001.
Values may be sent and summed in bfloat16 or wider, within the bound.
A program may use at most 128 MiB of HBM per device.

v0:
```python
import jax
import jax.numpy as jnp
from jax import lax
from jax.sharding import Mesh
from jax.sharding import PartitionSpec as P

DP = ("dp_0", "dp_1")
DP_VOCAB = ("dp_0", "dp_1", "vocab")


def sent_together(arrays, axis, split_dim, concat_dim, along):
    ends, at = ([], 0)
    for a in arrays[:-1]:
        at += a.shape[along]
        ends.append(at)
    both = jnp.concatenate(arrays, axis=along)
    return tuple(
        jnp.split(
            lax.all_to_all(both, axis, split_axis=split_dim, concat_axis=concat_dim, tiled=True),
            ends,
            axis=along,
        )
    )


def whole_of(shard, axes, dim):
    if not axes:
        return shard
    nearer = lax.all_gather(shard, axes[-1], axis=dim, tiled=True)
    return whole_of(nearer, axes[:-1], dim)


def on_device(hidden, tokens, old_weight, new_weight):
    ranks = lax.axis_size("vocab")
    rank = lax.axis_index("vocab")
    vocab_rows = old_weight.shape[0]
    first_id = rank * vocab_rows
    own_rows = hidden.shape[0]
    logits = lax.dot_general(
        lax.all_gather(hidden, "vocab", axis=0, tiled=True),
        old_weight,
        (((1,), (1,)), ((), ())),
        preferred_element_type=jnp.float32,
    )
    highest = jnp.max(logits, axis=1)
    summed = jnp.sum(jnp.exp(logits - highest[:, None]), axis=1)
    wanted = tokens - first_id
    columns = lax.broadcasted_iota(jnp.int32, logits.shape, 1)
    target = jnp.sum(jnp.where(columns == wanted[:, None], logits, 0.0), axis=1)
    stats = jnp.stack([highest, summed, target], axis=0)
    highest, summed, target = (stats[0], stats[1], stats[2])
    shaped = (
        highest.reshape(ranks, own_rows),
        summed.reshape(ranks, own_rows),
        target.reshape(ranks, own_rows),
    )
    got_high, got_sum, got_target = sent_together(
        (shaped[0], shaped[1], shaped[2]), "vocab", 0, 0, 1
    )
    highest = jnp.max(got_high, axis=0)
    summed = jnp.sum(got_sum * jnp.exp(got_high - highest[None, :]), axis=0)
    target = jnp.sum(got_target, axis=0)
    logprob = target - highest - jnp.log(summed)
    replicas = lax.axis_size(DP)
    trainer_cols = new_weight.shape[1]
    owned = lax.all_to_all(
        lax.all_to_all(new_weight, DP, split_axis=1, concat_axis=0, tiled=True),
        "vocab",
        split_axis=0,
        concat_axis=1,
        tiled=True,
    )
    owner_count = owned.shape[0]
    shaped_pieces = owned.reshape(owner_count, ranks, 1, trainer_cols // replicas)
    complete = whole_of(shaped_pieces, DP, 2)
    engine_weight = complete.reshape(owner_count, ranks * trainer_cols)
    return (logprob, engine_weight)


def solution(mesh):
    finer = Mesh(mesh.devices.reshape(4, 2, mesh.shape["vocab"]), ("dp_0", "dp_1", "vocab"))
    return jax.shard_map(
        on_device,
        mesh=finer,
        in_specs=(P(DP_VOCAB, None), P(DP), P("vocab", None), P(DP, "vocab")),
        out_specs=(P(DP_VOCAB), P("vocab", None)),
        check_vma=False,
    )
```

profile of v0, /device:TPU:1, one launch (start us, length us, event | category | flops | bytes accessed | tf_op | source)
XLA Modules:
  0.0 325.5 jit_solution(2934551947676968886)
XLA Ops:
  7.2 0.0 all-gather.9.cloned.1.call-start
  7.2 24.7 %all_to_all.44 = bf16[2304,8,40]{0,2,1:T(8,128)(2,1)S(1)} all-to-all(bf16[2304,8,40]{0,2,1:T(8,128)(2,1)} %bitcast.16), channel_id=1, replica_groups=mesh['dp_0'=4,'dp_1'=2,'vocab'=16] {'dp_0','dp_1'}, dimensions={1} | all-to-all | bytes 2949120 | tf_op jit(solution)/shard_map/all_to_all | solution.py:67
  31.9 0.2 copy.9
  32.2 0.5 all_to_all.38
  32.7 0.3 copy.10
  33.0 31.0 %all_to_all.45 = bf16[16,1152,40]{1,2,0:T(8,128)(2,1)S(1)} all-to-all(bf16[16,1152,40]{1,2,0:T(8,128)(2,1)S(1)} %copy.10), channel_id=1, replica_groups=mesh['dp_0'=4,'dp_1'=2,'vocab'=16] {'vocab'}, dimensions={0} | all-to-all | bytes 2949120 | tf_op jit(solution)/shard_map/all_to_all | solution.py:66
  64.0 1.3 copy.11
  65.2 0.0 all-gather.9.cloned.1.call-update
  65.2 0.0 copy-start
  65.3 0.0 all-gather.5.cloned.1.call-start
  65.3 0.7 all-gather.5.cloned.1.call-update
  66.0 0.0 all-gather.7.cloned.1.call-start
  66.1 40.3 %all-gather.9.cloned.1.call-done = bf16[1152,16,80]{0,1,2:T(8,128)(2,1)} async-done(((bf16[1152,16,40]{0,1,2:T(8,128)(2,1)}), bf16[1152,16,80]{0,1,2:T(8,128)(2,1)}) %all-gather.9.cloned.1.call-update) | async-done | bytes 2949136 | tf_op jit(solution)/shard_map/all_gather | solution.py:29
  106.3 4.0 %copy.12 = bf16[1152,16,80]{0,2,1:T(8,128)(2,1)} copy(bf16[1152,16,80]{0,1,2:T(8,128)(2,1)} %all-gather.9.cloned.1.call-done) | data formatting | bytes 5898240 | tf_op jit(solution)/shard_map/all_gather | solution.py:29
  110.3 0.0 all-gather.7.cloned.1.call-update
  110.3 0.0 copy-done
  110.4 81.7 %all-gather.5.cloned.1.call-done = bf16[1024,5120]{1,0:T(8,128)(2,1)} async-done(((bf16[64,5120]{1,0:T(8,128)(2,1)}), bf16[1024,5120]{1,0:T(8,128)(2,1)}) %all-gather.5.cloned.1.call-update) | async-done | bytes 10485776 | tf_op jit(solution)/shard_map/all_gather | solution.py:40
  192.1 19.5 %fusion.1 = (f32[1024]{0:T(1024)S(1)}, f32[1024,1152]{1,0:T(8,128)}) fusion(bf16[1024,5120]{1,0:T(8,128)(2,1)} %all-gather.5.cloned.1.call-done, bf16[1152,5120]{1,0:T(8,128)(2,1)} %param.6), kind=kOutput, calls=%fused_computation.11 | convolution fusion | flops 12080774144 | bytes 27004928 | tf_op jit(solution)/shard_map/dot_general | solution.py:39
  211.5 0.1 reshape_squeeze_stack.9
  211.6 3.1 exponential_reduce_fusion
  214.8 0.1 reshape_squeeze_stack.10
  214.8 0.1 reshape_squeeze_stack.11
  214.9 0.1 pad_maximum_fusion
  215.0 10.4 %all_to_all.46 = f32[16,1,192]{2,1,0:T(1,128)S(1)} all-to-all(f32[16,1,192]{2,1,0:T(1,128)S(1)} %all_to_all.32), channel_id=1, replica_groups=mesh['dp_0'=4,'dp_1'=2,'vocab'=16] {'vocab'}, dimensions={0} | all-to-all | bytes 24576 | tf_op jit(solution)/shard_map/all_to_all | solution.py:19
  225.4 0.1 slice_reduce_fusion
  225.5 0.5 log_subtract_fusion
  226.0 76.7 %all-gather.7.cloned.1.call-done = bf16[1152,16,8,40]{0,3,2,1:T(8,128)(2,1)} async-done(((bf16[1152,16,2,40]{0,3,2,1:T(8,128)(2,1)}), bf16[1152,16,8,40]{0,3,2,1:T(8,128)(2,1)}) %all-gather.7.cloned.1.call-update) | async-done | bytes 11796496 | tf_op jit(solution)/shard_map/all_gather | solution.py:29
  302.7 16.3 %copy.13 = bf16[1152,5120]{1,0:T(8,128)(2,1)} copy(bf16[1152,5120]{0,1:T(8,128)(2,1)} %bitcast.12) | data formatting | bytes 23592960
  (4 shorter events, 0.0 us)
Async XLA Ops:
  7.2 99.1 %all-gather.9.cloned.1.call-start = ((), (), s32[]{:S(2)}) async-start(), calls=%async_computation.5 | async-start | bytes 4423680 | tf_op jit(solution)/shard_map/all_gather | solution.py:29
  65.2 45.1 %copy-start = (s32[1024]{0:T(1024)S(1)}, s32[1024]{0:T(1024)}, u32[]{:S(2)}) copy-start(s32[1024]{0:T(1024)} %param.5) | copy-start | bytes 12292
  65.3 126.8 %all-gather.5.cloned.1.call-start = ((), (), s32[]{:S(2)}) async-start(), calls=%async_computation.3 | async-start | bytes 11141120 | tf_op jit(solution)/shard_map/all_gather | solution.py:40
  66.0 236.7 %all-gather.7.cloned.1.call-start = ((), (), s32[]{:S(2)}) async-start(), calls=%async_computation.4 | async-start | bytes 14745600 | tf_op jit(solution)/shard_map/all_gather | solution.py:29
Sparse Core Ops, SparseCore 0:
  65.4 40.8 all-gather.8
  108.8 83.2 all-gather.4
  193.7 108.8 all-gather.6
where the time goes:
time: 326 us; the launch traced here: 325 us
  waiting for transfers between devices  199 us (61%)
  blocking collectives  66 us (20%)
  local copies, waits for them, and re-layouts  22.8 us (7%)
  matrix products  19.5 us (6%)
  between operations  13.8 us (4%)
  other arithmetic  3.87 us (1%)
    all_gather x2, waiting for transfers between devices, whole_of(): nearer = lax.all_gather(shard, axes[-1], axis=dim, tiled=True)  117 us
    all_gather x1, waiting for transfers between devices, on_device(): lax.all_gather(hidden, 'vocab', axis=0, tiled=True)  81.7 us
    all_to_all x1, blocking collectives, on_device(): lax.all_to_all(lax.all_to_all(new_weight, DP, split_axis=1, concat_axis=0...  31 us
    all_to_all x1, blocking collectives, on_device(): lax.all_to_all(new_weight, DP, split_axis=1, concat_axis=0, tiled=True)  24.7 us
    dot_general x1, matrix products, on_device(): lax.dot_general(lax.all_gather(hidden, 'vocab', axis=0, tiled=True), old_...  19.5 us
    unnamed x4, local copies, waits for them, and re-layouts  16.3 us
    all_to_all x1, blocking collectives, sent_together(): lax.all_to_all(both, axis, split_axis=split_dim, concat_axis=concat_dim,...  10.4 us
  transfers between devices with their start and end apart: 3, of which 3 were waited for; matrix products, arithmetic and copies ran while one was open for 8% of the time, Pallas kernels for 0%

commit v1 on v0

--- a/solution.py
+++ b/solution.py
@@ -37,7 +37,9 @@
     first_id = rank * vocab_rows
     own_rows = hidden.shape[0]
     logits = lax.dot_general(
-        lax.all_gather(hidden, "vocab", axis=0, tiled=True),
+        jnp.concatenate(
+            lax.all_to_all(jnp.stack([hidden] * lax.axis_size("vocab")), "vocab", 0, 0), axis=0
+        ),
         old_weight,
         (((1,), (1,)), ((), ())),
         preferred_element_type=jnp.float32,

time: 326 us -> 300 us (0.920)
  waiting for transfers between devices: 199 us -> 159 us
  starting transfers between devices: 0.12 us -> 7.64 us
  local copies, waits for them, and re-layouts: 22.8 us -> 28.2 us
    all_to_all x0 -> x1, waiting for transfers between devices: none -> 118 us  [on_device(): lax.all_to_all(jnp.stack([hidden] * lax.axis_size('vocab')), 'vocab', 0, 0)]
    all_gather x1 -> x0, waiting for transfers between devices: 81.7 us -> none  [on_device(): lax.all_gather(hidden, 'vocab', axis=0, tiled=True)]
    all_gather x2, waiting for transfers between devices: 117 us -> 41 us  [whole_of(): nearer = lax.all_gather(shard, axes[-1], axis=dim, tiled=True)]
    all_to_all x0 -> x1, starting transfers between devices: none -> 7.57 us  [on_device(): lax.all_to_all(jnp.stack([hidden] * lax.axis_size('vocab')), 'vocab', 0, 0)]
    another operation x0 -> x1, local copies, waits for them, and re-layouts: none -> 5.4 us  [on_device(): jnp.stack([hidden] * lax.axis_size('vocab'))]
    unnamed x4 -> x6, local copies, waits for them, and re-layouts: 16.3 us -> 16.3 us
  transfers between devices with their start and end apart: 3 -> 3, of which waited for: 3 -> 2; matrix products, arithmetic and copies ran while one was open for 8% -> 10% of each run, Pallas kernels for 0% -> 0%
where the time goes in v1:
time: 300 us; the launch traced here: 299 us
  waiting for transfers between devices  159 us (53%)
  blocking collectives  66.9 us (22%)
  local copies, waits for them, and re-layouts  28.2 us (9%)
  matrix products  19.5 us (6%)
  between operations  14.1 us (5%)
  starting transfers between devices  7.64 us (3%)
  other arithmetic  3.87 us (1%)
    all_to_all x1, waiting for transfers between devices, on_device(): lax.all_to_all(jnp.stack([hidden] * lax.axis_size('vocab')), 'vocab', 0, 0)  118 us
    all_gather x2, waiting for transfers between devices, whole_of(): nearer = lax.all_gather(shard, axes[-1], axis=dim, tiled=True)  41 us
    all_to_all x1, blocking collectives, on_device(): lax.all_to_all(lax.all_to_all(new_weight, DP, split_axis=1, concat_axis=0...  31 us
    all_to_all x1, blocking collectives, on_device(): lax.all_to_all(new_weight, DP, split_axis=1, concat_axis=0, tiled=True)  24.7 us
    dot_general x1, matrix products, on_device(): lax.dot_general(jnp.concatenate(lax.all_to_all(jnp.stack([hidden] * lax.a...  19.5 us
    unnamed x6, local copies, waits for them, and re-layouts  16.3 us
    all_to_all x1, blocking collectives, sent_together(): lax.all_to_all(both, axis, split_axis=split_dim, concat_axis=concat_dim,...  11.2 us
    all_to_all x1, starting transfers between devices, on_device(): lax.all_to_all(jnp.stack([hidden] * lax.axis_size('vocab')), 'vocab', 0, 0)  7.57 us
  transfers between devices with their start and end apart: 3, of which 2 were waited for; matrix products, arithmetic and copies ran while one was open for 10% of the time, Pallas kernels for 0%

profile of v1, /device:TPU:1, one launch (start us, length us, event | category | flops | bytes accessed | tf_op | source)
XLA Modules:
  0.0 299.5 jit_solution(362709147990168644)
XLA Ops:
  7.2 0.0 all-gather.6.cloned.1.call-start
  7.2 24.7 %all_to_all.49 = bf16[2304,8,40]{0,2,1:T(8,128)(2,1)S(1)} all-to-all(bf16[2304,8,40]{0,2,1:T(8,128)(2,1)} %bitcast.17), channel_id=1, replica_groups=mesh['dp_0'=4,'dp_1'=2,'vocab'=16] {'dp_0','dp_1'}, dimensions={1} | all-to-all | bytes 2949120 | tf_op jit(solution)/shard_map/all_to_all | solution.py:69
  31.9 0.2 copy.9
  32.2 0.5 all_to_all.42
  32.7 0.3 copy.10
  33.0 31.0 %all_to_all.50 = bf16[16,1152,40]{1,2,0:T(8,128)(2,1)S(1)} all-to-all(bf16[16,1152,40]{1,2,0:T(8,128)(2,1)S(1)} %copy.10), channel_id=1, replica_groups=mesh['dp_0'=4,'dp_1'=2,'vocab'=16] {'vocab'}, dimensions={0} | all-to-all | bytes 2949120 | tf_op jit(solution)/shard_map/all_to_all | solution.py:68
  64.0 1.3 copy.11
  65.2 0.0 all-gather.6.cloned.1.call-update
  65.2 0.0 copy-start
  65.3 0.0 all-gather.4.cloned.1.call-start
  65.3 41.0 %all-gather.6.cloned.1.call-done = bf16[1152,16,80]{0,1,2:T(8,128)(2,1)} async-done(((bf16[1152,16,40]{0,1,2:T(8,128)(2,1)}), bf16[1152,16,80]{0,1,2:T(8,128)(2,1)}) %all-gather.6.cloned.1.call-update) | async-done | bytes 2949136 | tf_op jit(solution)/shard_map/all_gather | solution.py:29
  106.3 4.0 %copy.12 = bf16[1152,16,80]{0,2,1:T(8,128)(2,1)} copy(bf16[1152,16,80]{0,1,2:T(8,128)(2,1)} %all-gather.6.cloned.1.call-done) | data formatting | bytes 5898240 | tf_op jit(solution)/shard_map/all_gather | solution.py:29
  110.3 0.0 all-gather.4.cloned.1.call-update
  110.3 0.0 copy-done
  110.3 5.4 %stack.2 = bf16[16,64,5120]{2,1,0:T(8,128)(2,1)} broadcast(bf16[64,5120]{1,0:T(8,128)(2,1)S(1)} %copy-done), dimensions={1,2} | broadcast | bytes 11141120 | tf_op jit(solution)/shard_map/stack | solution.py:41
  115.7 0.0 copy-start.1
  115.7 7.6 %all-to-all-start = ((bf16[16,64,5120]{2,1,0:T(8,128)(2,1)}), bf16[16,64,5120]{2,1,0:T(8,128)(2,1)}, u32[]{:S(2)}, u32[]{:S(2)}) async-start(bf16[16,64,5120]{2,1,0:T(8,128)(2,1)} %stack.2), calls=%async_computation | async-start | bytes 20971520 | tf_op jit(solution)/shard_map/all_to_all | solution.py:41
  123.3 0.0 copy-done.1
  123.3 118.3 %all-to-all-done = bf16[16,64,5120]{2,1,0:T(8,128)(2,1)} async-done(((bf16[16,64,5120]{2,1,0:T(8,128)(2,1)}), bf16[16,64,5120]{2,1,0:T(8,128)(2,1)}, u32[]{:S(2)}, u32[]{:S(2)}) %all-to-all-start) | async-done | bytes 10485792 | tf_op jit(solution)/shard_map/all_to_all | solution.py:41
  241.6 19.5 %fusion.1 = (f32[1024]{0:T(1024)S(1)}, f32[1024,1152]{1,0:T(8,128)}) fusion(bf16[1024,5120]{1,0:T(8,128)(2,1)} %bitcast, bf16[1152,5120]{1,0:T(8,128)(2,1)} %param.6), kind=kOutput, calls=%fused_computation.11 | convolution fusion | flops 12080774144 | bytes 27004928 | tf_op jit(solution)/shard_map/dot_general | solution.py:39
  261.1 0.1 reshape_squeeze_stack.9
  261.2 3.1 %exponential_reduce_fusion = (f32[1024]{0:T(1024)S(1)}, f32[1024]{0:T(1024)S(1)}) fusion(f32[1024,1152]{1,0:T(8,128)} %get-tuple-element.11, f32[1024]{0:T(1024)S(1)} %get-tuple-element.10, s32[1024]{0:T(1024)S(1)} %broadcast_subtract_fusion), kind=kLoop, calls=%fused_computation.2 | loop fusion | flops 5896192 | bytes 4734976 | tf_op jit(solution)/shard_map/reduce_sum | solution.py:48
  264.3 0.1 reshape_squeeze_stack.10
  264.4 0.1 reshape_squeeze_stack.11
  264.5 0.1 pad_maximum_fusion
  264.6 11.2 %all_to_all.51 = f32[16,1,192]{2,1,0:T(1,128)S(1)} all-to-all(f32[16,1,192]{2,1,0:T(1,128)S(1)} %all_to_all.36), channel_id=1, replica_groups=mesh['dp_0'=4,'dp_1'=2,'vocab'=16] {'vocab'}, dimensions={0} | all-to-all | bytes 24576 | tf_op jit(solution)/shard_map/all_to_all | solution.py:19
  275.8 0.1 slice_reduce_fusion
  275.8 0.5 log_subtract_fusion
  276.4 0.0 all-gather.4.cloned.1.call-done
  276.4 16.3 %copy.13 = bf16[1152,5120]{1,0:T(8,128)(2,1)} copy(bf16[1152,5120]{0,1:T(8,128)(2,1)} %bitcast.13) | data formatting | bytes 23592960
  (4 shorter events, 0.0 us)
Async XLA Ops:
  7.2 99.1 %all-gather.6.cloned.1.call-start = ((), (), s32[]{:S(2)}) async-start(), calls=%async_computation.5 | async-start | bytes 4423680 | tf_op jit(solution)/shard_map/all_gather | solution.py:29
  65.2 45.1 %copy-start = (bf16[64,5120]{1,0:T(8,128)(2,1)S(1)}, bf16[64,5120]{1,0:T(8,128)(2,1)}, u32[]{:S(2)}) copy-start(bf16[64,5120]{1,0:T(8,128)(2,1)} %param.4) | copy-start | bytes 1966084
  65.3 211.1 %all-gather.4.cloned.1.call-start = ((), (), s32[]{:S(2)}) async-start(), calls=%async_computation.4 | async-start | bytes 14745600 | tf_op jit(solution)/shard_map/all_gather | solution.py:29
  115.7 7.6 %copy-start.1 = (s32[1024]{0:T(1024)S(1)}, s32[1024]{0:T(1024)}, u32[]{:S(2)}) copy-start(s32[1024]{0:T(1024)} %param.5) | copy-start | bytes 12292
  115.7 125.9 %all-to-all-start = ((bf16[16,64,5120]{2,1,0:T(8,128)(2,1)}), bf16[16,64,5120]{2,1,0:T(8,128)(2,1)}, u32[]{:S(2)}, u32[]{:S(2)}) async-start(bf16[16,64,5120]{2,1,0:T(8,128)(2,1)} %stack.2), calls=%async_computation | async-start | bytes 20971520 | tf_op jit(solution)/shard_map/all_to_all | solution.py:41
Sparse Core Ops, SparseCore 0:
  65.4 40.8 all-gather.5
  110.4 112.8 all-gather.3
